TPU v7x, 128 devices: a whole 4x4x4 slice. The times are simulated.
128 devices in a mesh: grp: 8 (over y_hi, z), pair: 16 (over x, y_lo, core).
Axes of the slice: x: 4, y: 4 (y_hi: 2, y_lo: 2; y = y_hi * 2 + y_lo), z: 4, core: 2. Of those that a mesh axis runs over, the one named last changes fastest.
Arguments:
- amplitudes: bfloat16 [128, 512, 512], P('pair', 'grp'), may hold values from -6 to 6
- cholesky: bfloat16 [512, 512, 2048], P('pair', 'grp'), may hold values from -0.09375 to 0.09375
Outputs:
- ladder_term: float32 [512, 4, 128], P('pair', None, 'grp')
All inputs are finite; a program needn't handle non-finite values.
Results may differ from a plain program's by a relative error of at most 0.003.
Values may be sent and summed in bfloat16 or wider, within the bound.
A program may use at most 128 MiB of HBM per device.

v0:
```python
import jax
import jax.numpy as jnp
from jax import lax
from jax.sharding import PartitionSpec as P

A_WIN = 4


def from_root(x, axis, root):
    return lax.dynamic_index_in_dim(lax.all_gather(x, axis), root, 0, keepdims=False)


def split_up(x, dim, length):
    before, after = (x.shape[:dim], x.shape[dim + 1 :])
    return jnp.moveaxis(x.reshape(*before, length, -1, *after), dim, 0)


def sent_and_summed(x, axis, dim):
    length = lax.axis_size(axis)
    blocks = lax.all_to_all(split_up(x, dim, length), axis, 0, 0, tiled=True)
    return jnp.sum(blocks, axis=0)


def build_tile(chol_local, portion):
    return lax.dot_general(
        chol_local, portion, (((2,), (2,)), ((), ())), preferred_element_type=jnp.float32
    ).astype(jnp.bfloat16)


def ladder(integrals, amp_part):
    return lax.dot_general(
        integrals, amp_part, (((1, 3), (1, 2)), ((), ())), preferred_element_type=jnp.float32
    )


def per_device(amplitudes, cholesky):
    own_window = cholesky[:A_WIN]
    everyone = lax.all_gather(amplitudes, "pair", axis=0, tiled=True)
    shared = from_root(own_window, "pair", 0)
    summed = ladder(
        build_tile(cholesky, lax.all_gather(shared, "grp", axis=1, tiled=True)), everyone
    )
    return sent_and_summed(summed, "grp", 2)


def solution(mesh):
    in_specs = (P("pair", "grp", None), P("pair", "grp", None))
    out_specs = P("pair", None, "grp")
    return jax.shard_map(
        per_device, mesh=mesh, in_specs=in_specs, out_specs=out_specs, check_vma=False
    )
```

profile of v0, /device:TPU:0, one launch (start us, length us, event | category | flops | bytes accessed | tf_op | source)
XLA Modules:
  0.0 334.3 jit_solution(7351327069050586795)
XLA Ops:
  6.5 0.0 all-gather.9.cloned.1.call-start
  6.5 2.4 slice.4
  8.9 0.0 all-gather.9.cloned.1.call-update
  8.9 0.0 all-gather.7.cloned.1.call-start
  9.0 2.1 copy.7
  11.1 0.0 all-gather.7.cloned.1.call-update
  11.1 0.0 all-gather.11.cloned.1.call-start
  11.2 91.9 %all-gather.9.cloned.1.call-done = bf16[64,64,2048]{2,1,0:T(8,128)(2,1)} async-done(((bf16[4,64,2048]{2,1,0:T(8,128)(2,1)}), bf16[64,64,2048]{2,1,0:T(8,128)(2,1)}) %all-gather.9.cloned.1.call-update) | async-done | bytes 16777232 | tf_op jit(solution)/shard_map/all_gather | solution.py:10
  103.1 2.4 slice.6
  105.5 0.0 all-gather.11.cloned.1.call-update
  105.5 52.1 %all-gather.7.cloned.1.call-done = bf16[128,64,512]{2,0,1:T(8,128)(2,1)} async-done(((bf16[8,64,512]{2,0,1:T(8,128)(2,1)}), bf16[128,64,512]{2,0,1:T(8,128)(2,1)}) %all-gather.7.cloned.1.call-update) | async-done | bytes 8388624 | tf_op jit(solution)/shard_map/all_gather | solution.py:38
  157.6 110.0 %all-gather.11.cloned.1.call-done = bf16[4,512,2048]{2,1,0:T(8,128)(2,1)} async-done(((bf16[4,64,2048]{2,1,0:T(8,128)(2,1)}), bf16[4,512,2048]{2,1,0:T(8,128)(2,1)}) %all-gather.11.cloned.1.call-update) | async-done | bytes 8388624 | tf_op jit(solution)/shard_map/all_gather | solution.py:41
  267.6 47.5 %fusion.2 = f32[32,4,128,1]{0,2,3,1:T(8,128)S(1)} fusion(bf16[128,64,512]{2,0,1:T(8,128)(2,1)} %all-gather.7.cloned.1.call-done, bf16[4,512,2048]{2,1,0:T(8,128)(2,1)} %all-gather.11.cloned.1.call-done, bf16[32,64,2048]{2,1,0:T(8,128)(2,1)} %param.3), kind=kOutput, calls=%fused_computation.2 | convolution fusion | flops 18257805312 | bytes 25231360 | tf_op jit(solution)/shard_map/dot_general | solution.py:31
  315.1 0.2 reshape.13
  315.3 10.4 %all_to_all.5 = f32[8,1,2048]{2,1,0:T(1,128)S(1)} all-to-all(f32[8,1,2048]{2,1,0:T(1,128)S(1)} %reshape.13), channel_id=1, replica_groups=mesh['grp'=8,'pair'=16] {'grp'}, dimensions={0} | all-to-all | bytes 131072 | tf_op jit(solution)/shard_map/all_to_all | solution.py:20
  325.7 0.5 broadcast
  326.2 0.8 reduce
  327.0 0.1 reshape.14
  327.1 0.6 bitcast_reduce_fusion
  (1 shorter events, 0.0 us)
Async XLA Ops:
  6.5 96.6 %all-gather.9.cloned.1.call-start = ((), (), s32[]{:S(2)}) async-start(), calls=%async_computation.2 | async-start | bytes 17825792 | tf_op jit(solution)/shard_map/all_gather | solution.py:10
  8.9 148.7 %all-gather.7.cloned.1.call-start = ((), (), s32[]{:S(2)}) async-start(), calls=%async_computation.1 | async-start | bytes 8912896 | tf_op jit(solution)/shard_map/all_gather | solution.py:38
  11.1 256.4 %all-gather.11.cloned.1.call-start = ((), (), s32[]{:S(2)}) async-start(), calls=%async_computation.3 | async-start | bytes 9437184 | tf_op jit(solution)/shard_map/all_gather | solution.py:41
Sparse Core Ops, SparseCore 0:
  9.1 94.0 all-gather.8
  104.8 52.8 all-gather.6
  159.9 107.6 all-gather.10
where the time goes:
time: 335 us; the launch traced here: 334 us
  waiting for transfers between devices  254 us (76%)
  matrix products  47.5 us (14%)
  between operations  13.1 us (4%)
  blocking collectives  10.4 us (3%)
  local copies, waits for them, and re-layouts  7.68 us (2%)
    all_gather x1, waiting for transfers between devices, per_device(): lax.all_gather(shared, 'grp', axis=1, tiled=True)  110 us
    all_gather x1, waiting for transfers between devices, from_root(): lax.all_gather(x, axis)  91.9 us
    all_gather x1, waiting for transfers between devices, per_device(): everyone = lax.all_gather(amplitudes, 'pair', axis=0, tiled=True)  52.1 us
    dot_general x1, matrix products, ladder(): lax.dot_general(integrals, amp_part, (((1, 3), (1, 2)), ((), ())), prefer...  47.5 us
    all_to_all x1, blocking collectives, sent_and_summed(): blocks = lax.all_to_all(split_up(x, dim, length), axis, 0, 0, tiled=True)  10.4 us
  transfers between devices with their start and end apart: 3, of which 3 were waited for; matrix products, arithmetic and copies ran while one was open for 1% of the time, Pallas kernels for 0%

commit v1 on v0

--- a/solution.py
+++ b/solution.py
@@ -35,7 +35,10 @@
 
 def per_device(amplitudes, cholesky):
     own_window = cholesky[:A_WIN]
-    everyone = lax.all_gather(amplitudes, "pair", axis=0, tiled=True)
+    size = lax.axis_size("pair")
+    pieces = jnp.stack([amplitudes for _ in range(size)])
+    pieces = lax.all_to_all(pieces, "pair", split_axis=0, concat_axis=0)
+    everyone = jnp.concatenate(pieces, axis=0)
     shared = from_root(own_window, "pair", 0)
     summed = ladder(
         build_tile(cholesky, lax.all_gather(shared, "grp", axis=1, tiled=True)), everyone

time: 335 us -> 368 us (1.099)
  waiting for transfers between devices: 254 us -> 271 us
  matrix products: 47.5 us -> 54.3 us
  starting transfers between devices: 0.09 us -> 5.06 us
    all_gather x1, waiting for transfers between devices: 110 us -> 176 us  [per_device(): lax.all_gather(shared, 'grp', axis=1, tiled=True)]
    all_gather x1 -> x0, waiting for transfers between devices: 52.1 us -> none  [per_device(): everyone = lax.all_gather(amplitudes, 'pair', axis=0, tiled=True)]
    dot_general x0 -> x1, matrix products: none -> 39.1 us  [build_tile(): lax.dot_general(chol_local, portion, (((2,), (2,)), ((), ())), preferred_...]
    dot_general x1, matrix products: 47.5 us -> 15.1 us  [ladder(): lax.dot_general(integrals, amp_part, (((1, 3), (1, 2)), ((), ())), prefer...]
    another operation x0 -> x1, local copies, waits for them, and re-layouts: none -> 5.32 us  [per_device(): pieces = jnp.stack([amplitudes for _ in range(size)])]
    all_to_all x0 -> x1, starting transfers between devices: none -> 5.02 us  [per_device(): pieces = lax.all_to_all(pieces, 'pair', split_axis=0, concat_axis=0)]
  transfers between devices with their start and end apart: 3 -> 3, of which waited for: 3 -> 2; matrix products, arithmetic and copies ran while one was open for 1% -> 12% of each run, Pallas kernels for 0% -> 0%
where the time goes in v1:
time: 368 us; the launch traced here: 366 us
  waiting for transfers between devices  271 us (74%)
  matrix products  54.3 us (15%)
  between operations  13.4 us (4%)
  local copies, waits for them, and re-layouts  10.8 us (3%)
  blocking collectives  10.6 us (3%)
  starting transfers between devices  5.06 us (1%)
    all_gather x1, waiting for transfers between devices, per_device(): lax.all_gather(shared, 'grp', axis=1, tiled=True)  176 us
    all_gather x1, waiting for transfers between devices, from_root(): lax.all_gather(x, axis)  94.2 us
    dot_general x1, matrix products, build_tile(): lax.dot_general(chol_local, portion, (((2,), (2,)), ((), ())), preferred_...  39.1 us
    dot_general x1, matrix products, ladder(): lax.dot_general(integrals, amp_part, (((1, 3), (1, 2)), ((), ())), prefer...  15.1 us
    all_to_all x1, blocking collectives, sent_and_summed(): blocks = lax.all_to_all(split_up(x, dim, length), axis, 0, 0, tiled=True)  10.6 us
  transfers between devices with their start and end apart: 3, of which 2 were waited for; matrix products, arithmetic and copies ran while one was open for 12% of the time, Pallas kernels for 0%

profile of v1, /device:TPU:0, one launch (start us, length us, event | category | flops | bytes accessed | tf_op | source)
XLA Modules:
  0.0 366.2 jit_solution(12319157586844353387)
XLA Ops:
  6.5 0.0 all-gather.6.cloned.1.call-start
  6.5 2.3 slice.4
  8.8 0.0 all-gather.6.cloned.1.call-update
  8.9 0.0 all-gather.8.cloned.1.call-start
  8.9 94.2 %all-gather.6.cloned.1.call-done = bf16[64,64,2048]{2,1,0:T(8,128)(2,1)} async-done(((bf16[4,64,2048]{2,1,0:T(8,128)(2,1)}), bf16[64,64,2048]{2,1,0:T(8,128)(2,1)}) %all-gather.6.cloned.1.call-update) | async-done | bytes 16777232 | tf_op jit(solution)/shard_map/all_gather | solution.py:10
  103.1 2.4 slice.6
  105.5 0.0 all-gather.8.cloned.1.call-update
  105.5 5.3 %stack.2 = bf16[16,8,64,512]{3,2,1,0:T(8,128)(2,1)} broadcast(bf16[8,64,512]{2,1,0:T(8,128)(2,1)} %param.2), dimensions={1,2,3} | broadcast | bytes 8912896 | tf_op jit(solution)/shard_map/stack | solution.py:39
  110.8 5.0 %all-to-all-start = ((bf16[16,8,64,512]{3,2,1,0:T(8,128)(2,1)}), bf16[16,8,64,512]{3,2,1,0:T(8,128)(2,1)}, u32[]{:S(2)}, u32[]{:S(2)}) async-start(bf16[16,8,64,512]{3,2,1,0:T(8,128)(2,1)} %stack.2), calls=%async_computation | async-start | bytes 16777216 | tf_op jit(solution)/shard_map/all_to_all | solution.py:40
  115.8 176.4 %all-gather.8.cloned.1.call-done = bf16[4,512,2048]{2,1,0:T(8,128)(2,1)} async-done(((bf16[4,64,2048]{2,1,0:T(8,128)(2,1)}), bf16[4,512,2048]{2,1,0:T(8,128)(2,1)}) %all-gather.8.cloned.1.call-update) | async-done | bytes 8388624 | tf_op jit(solution)/shard_map/all_gather | solution.py:44
  292.2 39.1 %fusion.31 = bf16[32,64,4,512,1]{3,0,1,4,2:T(8,128)(2,1)} fusion(bf16[4,512,2048]{2,1,0:T(8,128)(2,1)} %all-gather.8.cloned.1.call-done, bf16[32,64,2048]{2,1,0:T(8,128)(2,1)} %param.3), kind=kOutput, calls=%fused_computation.1.clone.clone.clone.1 | convolution fusion | flops 17184063488 | bytes 25165824 | tf_op jit(solution)/shard_map/dot_general | solution.py:25
  331.4 0.0 all-to-all-done
  331.4 15.1 %fusion.9 = f32[8,32,4,16]{1,3,0,2:T(8,128)S(1)} fusion(bf16[8,16,64,512]{3,2,1,0:T(8,128)(2,1)} %bitcast.5, bf16[32,64,4,512,1]{3,0,1,4,2:T(8,128)(2,1)} %fusion.31), kind=kOutput, calls=%fused_computation.9 | convolution fusion | flops 1073741824 | bytes 16842752 | tf_op jit(solution)/shard_map/dot_general | solution.py:31
  346.5 0.2 reshape.16
  346.7 10.6 %all_to_all.10 = f32[8,1,2048]{2,1,0:T(1,128)S(1)} all-to-all(f32[8,1,2048]{2,1,0:T(1,128)S(1)} %reshape.16), channel_id=1, replica_groups=mesh['grp'=8,'pair'=16] {'grp'}, dimensions={0} | all-to-all | bytes 131072 | tf_op jit(solution)/shard_map/all_to_all | solution.py:20
  357.3 0.5 broadcast.2
  357.8 0.8 reduce
  358.6 0.1 reshape.17
  358.8 0.6 bitcast_reduce_fusion
  (1 shorter events, 0.0 us)
Async XLA Ops:
  6.5 96.6 %all-gather.6.cloned.1.call-start = ((), (), s32[]{:S(2)}) async-start(), calls=%async_computation.2 | async-start | bytes 17825792 | tf_op jit(solution)/shard_map/all_gather | solution.py:10
  8.9 283.4 %all-gather.8.cloned.1.call-start = ((), (), s32[]{:S(2)}) async-start(), calls=%async_computation.3 | async-start | bytes 9437184 | tf_op jit(solution)/shard_map/all_gather | solution.py:44
  110.8 220.6 %all-to-all-start = ((bf16[16,8,64,512]{3,2,1,0:T(8,128)(2,1)}), bf16[16,8,64,512]{3,2,1,0:T(8,128)(2,1)}, u32[]{:S(2)}, u32[]{:S(2)}) async-start(bf16[16,8,64,512]{3,2,1,0:T(8,128)(2,1)} %stack.2), calls=%async_computation | async-start | bytes 16777216 | tf_op jit(solution)/shard_map/all_to_all | solution.py:40
Sparse Core Ops, SparseCore 0:
  9.0 94.0 all-gather.5
  105.6 186.5 all-gather.7
